TPU v7x, 256 devices: a whole 4x4x8 slice. The times are simulated.
256 devices in a mesh: row: 8 (over x, z_hi), col: 32 (over y, z_lo, core).
Axes of the slice: x: 4, y: 4, z: 8 (z_hi: 2, z_lo: 4; z = z_hi * 4 + z_lo), core: 2. Of those that a mesh axis runs over, the one named last changes fastest.
Arguments:
- symmetric: float32 [12288, 12288], P('row', 'col'), may hold values from -24 to 24, as said below
Outputs:
- reduced: float32 [12288, 12288], P('row', 'col')
Inputs may be any that keep to these rules, and one draw needn't show every extreme that they name: symmetric equals its transpose.
All inputs are finite; a program needn't handle non-finite values.
Results may differ from a plain program's by a relative error of at most 0.0001.
Values sent between devices are 32-bit elements; how exact they have to be, the bound alone decides.
No kernel may reach another device: no remote copies, remote signals or barrier semaphores. Data moves between devices by JAX's collectives and lax.ppermute only.
A program may use at most 64 MiB of HBM per device.

v0:
```python
import math
import jax
import jax.numpy as jnp
from jax import lax
from jax.sharding import Mesh
from jax.sharding import PartitionSpec as P

N = 12288
B = 256
ROW = ("row_0", "row_1")
COL = ("col_0", "col_1", "col_2")
HIGH = lax.Precision.HIGHEST


def padded_to(lines, size):
    spare = -len(lines) % size
    return jnp.pad(lines, [(0, spare)] + [(0, 0)] * (lines.ndim - 1))


def broadcast_by_parts(shard, axis, root):
    lines = jnp.where(lax.axis_index(axis) == root, shard, jnp.zeros_like(shard)).reshape(
        -1, *shard.shape[1:][-1:]
    )
    padded = padded_to(lines, lax.axis_size(axis))
    own = lax.psum_scatter(padded, axis, scatter_dimension=0, tiled=True)
    return lax.all_gather(own, axis, axis=0, tiled=True)[: len(lines)].reshape(shard.shape)


def broadcast_by_axis(shard, axes, root):
    shard = jnp.where(lax.axis_index(axes) == root, shard, jnp.zeros_like(shard))
    for axis in axes:
        shard = lax.psum(shard, axis)
    return shard


def in_blocks(shard, dim, size):
    dims = shard.shape
    parts = shard.reshape(*dims[:dim], size, dims[dim] // size, *dims[dim + 1 :])
    return jnp.moveaxis(parts, dim, 0)


def summed_on_arrival(shard, axis, dim):
    size = lax.axis_size(axis)
    parts = lax.all_to_all(in_blocks(shard, dim, size), axis, 0, 0, tiled=True)
    return jnp.sum(parts, axis=0)


def sum_in_two_steps(shard, axes, dim):
    far, near = axes
    own = summed_on_arrival(in_blocks(shard, dim, lax.axis_size(far)), near, dim + 1)
    return jnp.sum(lax.all_to_all(own, far, 0, 0, tiled=True), axis=0)


def from_everyone(shard, axis):
    size = lax.axis_size(axis)
    return lax.all_to_all(
        jnp.broadcast_to(shard[None], (size, *shard.shape)), axis, 0, 0, tiled=True
    )


def in_order(parts, dim):
    parts = jnp.moveaxis(parts, 0, dim)
    dims = parts.shape
    return parts.reshape(*dims[:dim], dims[dim] * dims[dim + 1], *dims[dim + 2 :])


def gather_axes(shard, axes, dim):
    far, near = axes
    parts = from_everyone(from_everyone(shard, far), near)
    return in_order(parts.swapaxes(0, 1).reshape(-1, *shard.shape), dim)


def total_of(shard, axes):
    lines = shard.reshape(-1, shard.shape[-1])
    own = sum_in_two_steps(
        padded_to(lines, lax.axis_size(axes[0]) * lax.axis_size(axes[1])), axes, 0
    )
    whole = gather_axes(own, axes, 0)
    return whole[: len(lines)].reshape(shard.shape)


def over_copies(shard, axis):
    return from_everyone(shard, axis).sum(axis=0)


def broadcast(shard, axis, root):
    return lax.dynamic_index_in_dim(lax.all_gather(shard, axis), root, 0, keepdims=False)


def contract(left_op, right_op, left_dim, right_dim):
    return lax.dot_general(
        left_op,
        right_op,
        (((left_dim,), (right_dim,)), ((), ())),
        precision=HIGH,
        preferred_element_type=jnp.float32,
    )


def per_device(symmetric):
    current = symmetric
    rows_dev, cols_dev = current.shape
    row_count_axis = lax.axis_size(ROW)
    col_count_axis = lax.axis_size(COL)
    row_at = lax.axis_index(ROW)
    col_at = lax.axis_index(COL)
    per_row = col_count_axis // row_count_axis
    global_rows = row_at * rows_dev + jnp.arange(rows_dev, dtype=jnp.int32)
    global_cols = col_at * cols_dev + jnp.arange(cols_dev, dtype=jnp.int32)
    band_index = jnp.arange(B, dtype=jnp.int32)
    identity = jnp.eye(B, dtype=jnp.float32)
    which = 0
    first_col = which * B
    below = first_col + B
    column_strip = broadcast_by_parts(current[:, first_col : first_col + B], COL, 0)
    panel_cols = jnp.where((global_rows >= below)[:, None], column_strip, jnp.float32(0.0))
    row_strip = broadcast_by_axis(current[first_col : first_col + B, :], ROW, 0)
    panel_trans = jnp.where((global_cols >= below)[None, :], row_strip, jnp.float32(0.0))
    gram_part = contract(panel_cols, panel_cols, 0, 0)
    leading_part = jnp.where(row_at == 0, panel_cols[below : below + B], jnp.float32(0.0))
    gram, leading_rows = lax.psum((gram_part, leading_part), ROW)
    lower_factor = jnp.linalg.cholesky(gram)
    basis_rows = lax.linalg.triangular_solve(
        lower_factor, panel_cols, left_side=False, lower=True, transpose_a=True
    )
    leading = lax.linalg.triangular_solve(
        lower_factor, leading_rows, left_side=False, lower=True, transpose_a=True
    )
    row_unit = (global_rows[:, None] - below == band_index[None, :]).astype(jnp.float32)
    reflector = basis_rows - row_unit
    col_unit = (band_index[:, None] == global_cols[None, :] - below).astype(jnp.float32)
    reflector_t = (
        lax.linalg.triangular_solve(lower_factor, panel_trans, left_side=True, lower=True)
        - col_unit
    )
    shifted = identity - leading
    normal_mat = contract(shifted, shifted, 0, 0)
    normal_chol = jnp.linalg.cholesky(normal_mat)
    interim = lax.linalg.triangular_solve(normal_chol, shifted.T, left_side=True, lower=True)
    t_mat = lax.linalg.triangular_solve(
        normal_chol, interim, left_side=True, lower=True, transpose_a=True
    )
    u_row = total_of(contract(current, reflector_t, 1, 1), (("col_0", "col_1"), "col_2"))
    core_sum = over_copies(contract(reflector, u_row, 0, 0), ROW)
    middle = contract(contract(t_mat, core_sum, 1, 0), t_mat, 1, 1)
    w_row = contract(u_row, t_mat, 1, 1) - 0.5 * contract(reflector, middle, 1, 0)
    offset = col_at % per_row * cols_dev
    w_piece = lax.dynamic_slice_in_dim(w_row, offset, cols_dev, 0)
    w_col = broadcast(w_piece, ROW, col_at // per_row)
    first_term = contract(reflector, w_col, 1, 1)
    second_term = contract(w_row, reflector_t, 1, 0)
    current = current - first_term - second_term
    factors = [lower_factor]
    inverse_root = jnp.float32(1.0 / math.sqrt(N))
    which = 0
    first_col = which * B
    below = first_col + B
    r_mat = factors[which].T * inverse_root
    old_strip = current[:, first_col : first_col + B]
    placed = jnp.zeros((rows_dev, B), jnp.float32).at[below : below + B].set(r_mat)
    inside = global_rows[:, None] < below + B
    updated = jnp.where(
        global_rows[:, None] >= below, jnp.where(inside, placed, jnp.float32(0.0)), old_strip
    )
    updated = jnp.where(col_at == 0, updated, old_strip)
    current = current.at[:, first_col : first_col + B].set(updated)
    old_top = current[first_col : first_col + B, :]
    onehot = (global_cols[:, None] - below == band_index[None, :]).astype(jnp.float32)
    mirror = contract(r_mat, onehot, 0, 1)
    new_top = jnp.where((global_cols >= below)[None, :], mirror, old_top)
    new_top = jnp.where(row_at == 0, new_top, old_top)
    current = current.at[first_col : first_col + B, :].set(new_top)
    return current


def solution(mesh):
    split = Mesh(mesh.devices.reshape(4, 2, 4, 4, 2), ("row_0", "row_1", "col_0", "col_1", "col_2"))
    return jax.shard_map(
        per_device, mesh=split, in_specs=(P(ROW, COL),), out_specs=P(ROW, COL), check_vma=False
    )
```

profile of v0, /device:TPU:1, one launch (start us, length us, event | category | flops | bytes accessed | tf_op | source)
XLA Modules:
  0.0 691.2 jit_solution(5647719800519934500)
XLA Ops:
  7.4 2.0 copy.58
  10.8 3.0 copy.70
  14.8 145.9 %reduce-scatter.4.cloned.1.call-done = f32[48,256]{1,0:T(8,128)} async-done(((f32[1536,256]{1,0:T(8,128)}), f32[48,256]{1,0:T(8,128)}) %reduce-scatter.4.cloned.1.call-update) | async-done | bytes 49168 | tf_op jit(solution)/shard_map/reduce_scatter | solution.py:25
  161.3 74.1 %all-gather.4.cloned.1.call-done = f32[1536,256]{1,0:T(8,128)} async-done(((f32[48,256]{1,0:T(8,128)}), f32[1536,256]{1,0:T(8,128)}) %all-gather.4.cloned.1.call-update) | async-done | bytes 1572880 | tf_op jit(solution)/shard_map/all_gather | solution.py:26
  238.1 2.1 fusion.67
  241.5 105.0 %all-reduce.11.cloned.1.call-done = (f32[256,256]{0,1:T(8,128)}, f32[256,256]{0,1:T(8,128)}) async-done(((f32[256,256]{0,1:T(8,128)}, f32[256,256]{0,1:T(8,128)}), (f32[256,256]{0,1:T(8,128)}, f32[256,256]{0,1:T(8,128)})) %all-reduce.11.cloned.1.call-update) | async-done | bytes 524304 | tf_op jit(solution)/shard_map/psum | solution.py:121
  348.6 11.7 %cholesky.130 = f32[128,128]{1,0:T(8,128)S(1)} custom-call(f32[128,128]{1,0:T(8,128)S(1)} %cholesky.194), custom_call_target="Cholesky" | custom-call | tf_op jit(solution)/shard_map/jit(cholesky)/cholesky | solution.py:122
  360.4 9.8 %custom-call.23 = f32[1,128,128]{1,2,0:T(8,128)S(1)} custom-call(f32[1,128,128]{2,1,0:T(8,128)S(1)} %get-tuple-element.89), custom_call_target="InvertDiagBlocksLowerTriangular" | custom-call | tf_op jit(solution)/shard_map/jit(cholesky)/cholesky | solution.py:122
  370.7 11.9 %cholesky.147 = f32[128,128]{1,0:T(8,128)S(1)} custom-call(f32[128,128]{1,0:T(8,128)S(1)} %convolution_subtract_fusion.8), custom_call_target="Cholesky" | custom-call | tf_op jit(solution)/shard_map/jit(cholesky)/cholesky | solution.py:122
  385.3 4.0 while.5
  389.3 19.7 %custom-call.20 = f32[2,128,128]{1,2,0:T(8,128)S(1)} custom-call(f32[2,128,128]{2,1,0:T(8,128)S(1)} %get-tuple-element.49), custom_call_target="InvertDiagBlocksLowerTriangular" | custom-call | tf_op jit(solution)/shard_map/triangular_solve | solution.py:123
  411.0 5.5 convolution_bitcast_fusion
  418.6 12.3 %all_to_all.25 = f32[2,16,48,256]{3,2,1,0:T(8,128)S(1)} all-to-all(f32[2,16,48,256]{3,2,1,0:T(8,128)S(1)} %copy.53), channel_id=1, replica_groups=mesh['row_0'=4,'row_1'=2,'col_0'=4,'col_1'=4,'col_2'=2] {'col_2'}, dimensions={0} | all-to-all | bytes 3145728 | tf_op jit(solution)/shard_map/all_to_all | solution.py:44
  431.9 4.5 all-to-all-start.1
  436.8 21.0 %all-to-all-done.1 = f32[16,48,256]{2,1,0:T(8,128)S(1)} async-done(((f32[16,48,256]{2,1,0:T(8,128)}), f32[16,48,256]{2,1,0:T(8,128)S(1)}, u32[]{:S(2)}, u32[]{:S(2)}) %all-to-all-start.1) | async-done | bytes 786464 | tf_op jit(solution)/shard_map/all_to_all | solution.py:51
  458.9 4.5 all-to-all-start.2
  466.3 11.7 %cholesky.164 = f32[128,128]{1,0:T(8,128)S(1)} custom-call(f32[128,128]{1,0:T(8,128)S(1)} %cholesky.197), custom_call_target="Cholesky" | custom-call | tf_op jit(solution)/shard_map/jit(cholesky)/cholesky | solution.py:138
  480.6 4.2 all-to-all-done.2
  486.2 6.3 all_to_all.26
  495.8 4.3 all-to-all-start.4
  502.4 10.6 %custom-call.24 = f32[1,128,128]{1,2,0:T(8,128)S(1)} custom-call(f32[1,128,128]{2,1,0:T(8,128)} %get-tuple-element.85), custom_call_target="InvertDiagBlocksLowerTriangular" | custom-call | tf_op jit(solution)/shard_map/jit(cholesky)/cholesky | solution.py:138
  516.4 12.5 %cholesky.181 = f32[128,128]{1,0:T(8,128)S(1)} custom-call(f32[128,128]{1,0:T(8,128)} %convolution_subtract_fusion.7), custom_call_target="Cholesky" | custom-call | tf_op jit(solution)/shard_map/jit(cholesky)/cholesky | solution.py:138
  535.1 8.4 %while.6 = (s32[]{:T(128)}, f32[256,256]{1,0:T(8,128)}, s32[2,2]{1,0:T(2,128)}, f32[2,128,128]{2,1,0:T(8,128)}, s32[]{:T(128)}) while((s32[]{:T(128)}, f32[256,256]{1,0:T(8,128)}, s32[2,2]{1,0:T(2,128)}, f32[2,128,128]{2,1,0:T(8,128)}, s32[]{:T(128)}) %tuple.73), condition=%wide.while_cond.4, body=%wide.while_body.4.sunk | while | flops 2 | bytes 132205 | solution.py:140
  536.7 2.7 bitcast_dynamic-update-slice_fusion.5
  540.7 2.7 bitcast_dynamic-update-slice_fusion.5
  543.4 21.1 %custom-call.21 = f32[2,128,128]{1,2,0:T(8,128)} custom-call(f32[2,128,128]{2,1,0:T(8,128)} %get-tuple-element.57), custom_call_target="InvertDiagBlocksLowerTriangular" | custom-call | tf_op jit(solution)/shard_map/triangular_solve | solution.py:140
  571.3 2.6 fusion.22
  573.9 2.6 reduce_sum.29
  579.2 2.7 fusion
  584.7 88.7 %all-gather.6.cloned.1.call-done = f32[3072,256]{1,0:T(8,128)} async-done(((f32[384,256]{1,0:T(8,128)}), f32[3072,256]{1,0:T(8,128)}) %all-gather.6.cloned.1.call-update) | async-done | bytes 3145744 | tf_op jit(solution)/shard_map/all_gather | solution.py:87
  673.4 4.3 convolution_subtract_fusion.1
  677.7 2.2 convolution_subtract_fusion
  (138 shorter events, 59.8 us)
Async XLA Ops:
  7.4 153.3 %reduce-scatter.4.cloned.1.call-start = ((), (), s32[]{:S(2)}) async-start(), calls=%async_computation.10 | async-start | bytes 1622016 | tf_op jit(solution)/shard_map/reduce_scatter | solution.py:25
  9.4 4.5 copy-start
  13.8 146.9 %all-reduce.7.cloned.1.call-start = ((), (), s32[]{:S(2)}) async-start(), calls=%async_computation.7 | async-start | bytes 786432 | tf_op jit(solution)/shard_map/psum | solution.py:32
  14.7 220.7 %all-gather.4.cloned.1.call-start = ((), (), s32[]{:S(2)}) async-start(), calls=%async_computation.6 | async-start | bytes 1622016 | tf_op jit(solution)/shard_map/all_gather | solution.py:26
  160.6 79.7 %all-reduce.9.cloned.1.call-start = ((), (), s32[]{:S(2)}) async-start(), calls=%async_computation.8 | async-start | bytes 786432 | tf_op jit(solution)/shard_map/psum | solution.py:32
  161.2 185.3 %all-reduce.11.cloned.1.call-start = ((), (), s32[]{:S(2)}) async-start(), calls=%async_computation.11 | async-start | bytes 1048576 | tf_op jit(solution)/shard_map/psum | solution.py:121
  240.3 106.2 %copy-start.19 = (pred[384]{0:T(512)(128)(4,1)}, pred[384]{0:T(512)(128)(4,1)S(1)}, u32[]{:S(2)}) copy-start(pred[384]{0:T(512)(128)(4,1)S(1)} %fusion.51) | copy-start | bytes 1156
  382.6 6.7 copy-start.13
  389.3 21.0 %copy-start.4 = (f32[256,256]{1,0:T(8,128)}, f32[256,256]{1,0:T(8,128)S(1)}, u32[]{:S(2)}) copy-start(f32[256,256]{1,0:T(8,128)S(1)} %get-tuple-element.200) | copy-start | bytes 786436
  389.3 21.0 %copy-start.21 = (s32[2,2]{1,0:T(2,128)}, s32[2,2]{1,0:T(2,128)S(1)}, u32[]{:S(2)}) copy-start(s32[2,2]{1,0:T(2,128)S(1)} %get-tuple-element.221) | copy-start | bytes 52
  409.0 1.3 copy-start.9
  410.4 0.7 copy-start.7
  431.9 4.6 copy-start.10
  431.9 4.6 copy-start.18
  431.9 26.0 %all-to-all-start.1 = ((f32[16,48,256]{2,1,0:T(8,128)}), f32[16,48,256]{2,1,0:T(8,128)S(1)}, u32[]{:S(2)}, u32[]{:S(2)}) async-start(f32[16,48,256]{2,1,0:T(8,128)} %reduce_sum.27), calls=%async_computation.1 | async-start | bytes 1572864 | tf_op jit(solution)/shard_map/all_to_all | solution.py:51
  436.8 26.6 %copy-start.5 = (f32[256,256]{1,0:T(8,128)S(1)}, f32[256,256]{1,0:T(8,128)}, u32[]{:S(2)}) copy-start(f32[256,256]{1,0:T(8,128)} %copy-done.4) | copy-start | bytes 786436
  458.9 25.9 %all-to-all-start.2 = ((f32[16,48,256]{2,1,0:T(8,128)}), f32[16,48,256]{2,1,0:T(8,128)}, u32[]{:S(2)}, u32[]{:S(2)}) async-start(f32[16,48,256]{2,1,0:T(8,128)} %broadcast_in_dim.49), calls=%async_computation.2 | async-start | bytes 1572864 | tf_op jit(solution)/shard_map/all_to_all | solution.py:56
  465.0 13.9 %copy-start.12 = (f32[256,128]{0,1:T(8,128)}, f32[256,128]{0,1:T(8,128)S(1)}, u32[]{:S(2)}) copy-start(f32[256,128]{0,1:T(8,128)S(1)} %fusion.42) | copy-start | bytes 393220
  465.6 0.7 copy-start.16
  478.8 0.9 copy-start.11
  495.8 78.1 %all-to-all-start.4 = ((f32[8,256,256]{2,1,0:T(8,128)}), f32[8,256,256]{2,1,0:T(8,128)}, u32[]{:S(2)}, u32[]{:S(2)}) async-start(f32[8,256,256]{2,1,0:T(8,128)} %broadcast_in_dim.51), calls=%async_computation.4 | async-start | bytes 4194304 | tf_op jit(solution)/shard_map/all_to_all | solution.py:56
  500.1 173.2 %all-gather.6.cloned.1.call-start = ((), (), s32[]{:S(2)}) async-start(), calls=%async_computation.9 | async-start | bytes 3538944 | tf_op jit(solution)/shard_map/all_gather | solution.py:87
  564.5 4.4 copy-start.17
  570.6 0.6 copy-start.6
  573.9 5.3 copy-start.3
  581.9 1.2 copy-start.1
  673.4 4.3 copy-start.2
  673.4 4.3 copy-start.8
  677.7 2.2 copy-start.15
  680.0 1.0 copy-start.14
  680.0 1.0 copy-start.20
Sparse Core Ops, SparseCore 0:
  13.9 146.6 reduce-scatter.3
  162.5 72.8 all-gather.3
Sparse Core Ops, SparseCore 1:
  16.7 49.2 all-reduce.6
  163.7 49.2 all-reduce.8
  240.4 106.1 all-reduce.10
  584.0 89.3 all-gather.5
where the time goes:
time: 702 us; the launch traced here: 691 us
  waiting for transfers between devices  439 us (63%)
  other arithmetic  128 us (18%)
  matrix products  39.4 us (6%)
  local copies, waits for them, and re-layouts  33.4 us (5%)
  blocking collectives  18.6 us (3%)
  between operations  18.4 us (3%)
  starting transfers between devices  13.8 us (2%)
    reduce_scatter x1, waiting for transfers between devices, broadcast_by_parts(): own = lax.psum_scatter(padded, axis, scatter_dimension=0, tiled=True)  146 us
    psum x1, waiting for transfers between devices, per_device(): gram, leading_rows = lax.psum((gram_part, leading_part), ROW)  105 us
    all_gather x1, waiting for transfers between devices, broadcast(): lax.all_gather(shard, axis)  88.7 us
    all_gather x1, waiting for transfers between devices, broadcast_by_parts(): lax.all_gather(own, axis, axis=0, tiled=True)[:len(lines)]  74.1 us
    another operation x7, other arithmetic, per_device(): normal_chol = jnp.linalg.cholesky(normal_mat)  38.7 us
    another operation x6, other arithmetic, per_device(): lower_factor = jnp.linalg.cholesky(gram)  34.1 us
    dot_general x11, matrix products, contract(): lax.dot_general(left_op, right_op, (((left_dim,), (right_dim,)), ((), ())...  24.9 us
    another operation x2, other arithmetic, per_device(): lax.linalg.triangular_solve(normal_chol, interim, left_side=True, lower=T...  22.8 us
  transfers between devices with their start and end apart: 9, of which 6 were waited for; matrix products, arithmetic and copies ran while one was open for 14% of the time, Pallas kernels for 0%

commit v1 on v0

--- a/solution.py
+++ b/solution.py
@@ -118,7 +118,7 @@
     panel_trans = jnp.where((global_cols >= below)[None, :], row_strip, jnp.float32(0.0))
     gram_part = contract(panel_cols, panel_cols, 0, 0)
     leading_part = jnp.where(row_at == 0, panel_cols[below : below + B], jnp.float32(0.0))
-    gram, leading_rows = lax.psum((gram_part, leading_part), ROW)
+    gram, leading_rows = lax.psum(lax.psum((gram_part, leading_part), "row_0"), "row_1")
     lower_factor = jnp.linalg.cholesky(gram)
     basis_rows = lax.linalg.triangular_solve(
         lower_factor, panel_cols, left_side=False, lower=True, transpose_a=True

time: 702 us -> 694 us (0.989)
  waiting for transfers between devices: 439 us -> 447 us
    psum x3 -> x2, waiting for transfers between devices: 105 us -> 124 us  [the longest x1 77.7 us: per_device(): lax.psum(lax.psum((gram_part, leading_part), 'row_0'), 'row_1')]
    all_gather x1, waiting for transfers between devices: 74.1 us -> 62.1 us  [broadcast_by_parts(): lax.all_gather(own, axis, axis=0, tiled=True)[:len(lines)]]
  transfers between devices with their start and end apart: 9 -> 8, of which waited for: 6 -> 7; matrix products, arithmetic and copies ran while one was open for 14% -> 13% of each run, Pallas kernels for 0% -> 0%
where the time goes in v1:
time: 694 us; the launch traced here: 690 us
  waiting for transfers between devices  447 us (64%)
  other arithmetic  127 us (18%)
  matrix products  37.8 us (5%)
  local copies, waits for them, and re-layouts  33.7 us (5%)
  between operations  16.6 us (2%)
  starting transfers between devices  15.3 us (2%)
  blocking collectives  11.8 us (2%)
    reduce_scatter x1, waiting for transfers between devices, broadcast_by_parts(): own = lax.psum_scatter(padded, axis, scatter_dimension=0, tiled=True)  147 us
    all_gather x1, waiting for transfers between devices, broadcast(): lax.all_gather(shard, axis)  89.2 us
    psum x1, waiting for transfers between devices, per_device(): lax.psum(lax.psum((gram_part, leading_part), 'row_0'), 'row_1')  77.7 us
    all_gather x1, waiting for transfers between devices, broadcast_by_parts(): lax.all_gather(own, axis, axis=0, tiled=True)[:len(lines)]  62.1 us
    psum x1, waiting for transfers between devices, per_device(): lax.psum((gram_part, leading_part), 'row_0')  46.4 us
    another operation x7, other arithmetic, per_device(): normal_chol = jnp.linalg.cholesky(normal_mat)  38.8 us
    another operation x6, other arithmetic, per_device(): lower_factor = jnp.linalg.cholesky(gram)  34 us
    dot_general x11, matrix products, contract(): lax.dot_general(left_op, right_op, (((left_dim,), (right_dim,)), ((), ())...  23.2 us
  transfers between devices with their start and end apart: 8, of which 7 were waited for; matrix products, arithmetic and copies ran while one was open for 13% of the time, Pallas kernels for 0%

profile of v1, /device:TPU:1, one launch (start us, length us, event | category | flops | bytes accessed | tf_op | source)
XLA Modules:
  0.0 690.0 jit_solution(3180399342901911236)
XLA Ops:
  9.9 3.0 copy.70
  13.1 146.7 %reduce-scatter.4.cloned.1.call-done = f32[48,256]{1,0:T(8,128)} async-done(((f32[1536,256]{1,0:T(8,128)}), f32[48,256]{1,0:T(8,128)}) %reduce-scatter.4.cloned.1.call-update) | async-done | bytes 49168 | tf_op jit(solution)/shard_map/reduce_scatter | solution.py:25
  160.6 62.1 %all-gather.4.cloned.1.call-done = f32[1536,256]{1,0:T(8,128)} async-done(((f32[48,256]{1,0:T(8,128)}), f32[1536,256]{1,0:T(8,128)}) %all-gather.4.cloned.1.call-update) | async-done | bytes 1572880 | tf_op jit(solution)/shard_map/all_gather | solution.py:26
  224.7 2.1 fusion.67
  228.3 46.4 %all-reduce.7.cloned.1.call-done = (f32[256,256]{0,1:T(8,128)}, f32[256,384]{0,1:T(8,128)}, f32[256,256]{0,1:T(8,128)}) async-done(((f32[256,256]{0,1:T(8,128)}, f32[256,384]{0,1:T(8,128)}, f32[256,256]{0,1:T(8,128)}), (f32[256,256]{0,1:T(8,128)}, f32[256,384]{0,1:T(8,128)}, f32[256,256]{0,1:T(8,128)})) %all-reduce.7.cloned.1.call-update) | async-done | bytes 917520 | tf_op jit(solution)/shard_map/psum | solution.py:121
  274.8 77.7 %all-reduce.9.cloned.1.call-done = (f32[256,256]{0,1:T(8,128)}, f32[256,384]{0,1:T(8,128)}, f32[256,256]{0,1:T(8,128)}) async-done(((f32[256,256]{0,1:T(8,128)}, f32[256,384]{0,1:T(8,128)}, f32[256,256]{0,1:T(8,128)}), (f32[256,256]{0,1:T(8,128)}, f32[256,384]{0,1:T(8,128)}, f32[256,256]{0,1:T(8,128)})) %all-reduce.9.cloned.1.call-update) | async-done | bytes 917520 | tf_op jit(solution)/shard_map/psum | solution.py:121
  354.6 11.7 %cholesky.130 = f32[128,128]{1,0:T(8,128)S(1)} custom-call(f32[128,128]{1,0:T(8,128)S(1)} %cholesky.194), custom_call_target="Cholesky" | custom-call | tf_op jit(solution)/shard_map/jit(cholesky)/cholesky | solution.py:122
  366.3 9.8 %custom-call.23 = f32[1,128,128]{1,2,0:T(8,128)S(1)} custom-call(f32[1,128,128]{2,1,0:T(8,128)S(1)} %get-tuple-element.93), custom_call_target="InvertDiagBlocksLowerTriangular" | custom-call | tf_op jit(solution)/shard_map/jit(cholesky)/cholesky | solution.py:122
  376.6 11.7 %cholesky.147 = f32[128,128]{1,0:T(8,128)S(1)} custom-call(f32[128,128]{1,0:T(8,128)S(1)} %convolution_subtract_fusion.8), custom_call_target="Cholesky" | custom-call | tf_op jit(solution)/shard_map/jit(cholesky)/cholesky | solution.py:122
  391.2 4.0 while.5
  395.2 19.7 %custom-call.20 = f32[2,128,128]{1,2,0:T(8,128)S(1)} custom-call(f32[2,128,128]{2,1,0:T(8,128)S(1)} %get-tuple-element.49), custom_call_target="InvertDiagBlocksLowerTriangular" | custom-call | tf_op jit(solution)/shard_map/triangular_solve | solution.py:123
  417.1 3.9 convolution_bitcast_fusion
  423.0 5.5 all_to_all.25
  429.5 4.3 all-to-all-start.1
  434.2 21.0 %all-to-all-done.1 = f32[16,48,256]{2,1,0:T(8,128)S(1)} async-done(((f32[16,48,256]{2,1,0:T(8,128)}), f32[16,48,256]{2,1,0:T(8,128)S(1)}, u32[]{:S(2)}, u32[]{:S(2)}) %all-to-all-start.1) | async-done | bytes 786464 | tf_op jit(solution)/shard_map/all_to_all | solution.py:51
  456.3 4.5 all-to-all-start.2
  463.6 11.7 %cholesky.164 = f32[128,128]{1,0:T(8,128)S(1)} custom-call(f32[128,128]{1,0:T(8,128)S(1)} %cholesky.197), custom_call_target="Cholesky" | custom-call | tf_op jit(solution)/shard_map/jit(cholesky)/cholesky | solution.py:138
  477.9 4.2 all-to-all-done.2
  483.5 6.3 all_to_all.26
  493.1 5.5 all-to-all-start.4
  500.9 10.6 %custom-call.24 = f32[1,128,128]{1,2,0:T(8,128)S(1)} custom-call(f32[1,128,128]{2,1,0:T(8,128)} %get-tuple-element.89), custom_call_target="InvertDiagBlocksLowerTriangular" | custom-call | tf_op jit(solution)/shard_map/jit(cholesky)/cholesky | solution.py:138
  514.9 12.5 %cholesky.181 = f32[128,128]{1,0:T(8,128)S(1)} custom-call(f32[128,128]{1,0:T(8,128)} %convolution_subtract_fusion.7), custom_call_target="Cholesky" | custom-call | tf_op jit(solution)/shard_map/jit(cholesky)/cholesky | solution.py:138
  533.7 8.8 %while.6 = (s32[]{:T(128)}, f32[256,256]{1,0:T(8,128)}, s32[2,2]{1,0:T(2,128)}, f32[2,128,128]{2,1,0:T(8,128)}, s32[]{:T(128)}) while((s32[]{:T(128)}, f32[256,256]{1,0:T(8,128)}, s32[2,2]{1,0:T(2,128)}, f32[2,128,128]{2,1,0:T(8,128)}, s32[]{:T(128)}) %tuple.72), condition=%wide.while_cond.4, body=%wide.while_body.4.sunk | while | flops 2 | bytes 132205 | solution.py:140
  535.5 2.9 bitcast_dynamic-update-slice_fusion.5
  539.7 2.8 bitcast_dynamic-update-slice_fusion.5
  542.5 21.1 %custom-call.21 = f32[2,128,128]{1,2,0:T(8,128)} custom-call(f32[2,128,128]{2,1,0:T(8,128)} %get-tuple-element.57), custom_call_target="InvertDiagBlocksLowerTriangular" | custom-call | tf_op jit(solution)/shard_map/triangular_solve | solution.py:140
  570.4 2.6 fusion.22
  573.0 2.6 reduce_sum.29
  578.3 2.7 fusion
  583.9 89.2 %all-gather.6.cloned.1.call-done = f32[3072,256]{1,0:T(8,128)} async-done(((f32[384,256]{1,0:T(8,128)}), f32[3072,256]{1,0:T(8,128)}) %all-gather.6.cloned.1.call-update) | async-done | bytes 3145744 | tf_op jit(solution)/shard_map/all_gather | solution.py:87
  673.1 4.3 convolution_subtract_fusion.1
  677.5 2.2 convolution_subtract_fusion
  (139 shorter events, 61.0 us)
Async XLA Ops:
  6.5 153.2 %reduce-scatter.4.cloned.1.call-start = ((), (), s32[]{:S(2)}) async-start(), calls=%async_computation.8 | async-start | bytes 1622016 | tf_op jit(solution)/shard_map/reduce_scatter | solution.py:25
  8.6 151.3 %copy-start = (f32[1536,384]{0,1:T(8,128)}, f32[1536,384]{0,1:T(8,128)S(1)}, u32[]{:S(2)}) copy-start(f32[1536,384]{0,1:T(8,128)S(1)} %copy.58) | copy-start | bytes 7077892
  13.0 209.7 %all-gather.4.cloned.1.call-start = ((), (), s32[]{:S(2)}) async-start(), calls=%async_computation.6 | async-start | bytes 1622016 | tf_op jit(solution)/shard_map/all_gather | solution.py:26
  159.8 114.9 %all-reduce.7.cloned.1.call-start = ((), (), s32[]{:S(2)}) async-start(), calls=%async_computation.9 | async-start | bytes 1835008 | tf_op jit(solution)/shard_map/psum | solution.py:121
  227.6 124.9 %all-reduce.9.cloned.1.call-start = ((), (), s32[]{:S(2)}) async-start(), calls=%async_computation.10 | async-start | bytes 1835008 | tf_op jit(solution)/shard_map/psum | solution.py:121
  274.8 140.1 %copy-start.21 = (pred[384]{0:T(512)(128)(4,1)}, pred[384]{0:T(512)(128)(4,1)S(1)}, u32[]{:S(2)}) copy-start(pred[384]{0:T(512)(128)(4,1)S(1)} %fusion.51) | copy-start | bytes 1156
  354.6 60.4 %copy-start.19 = (f32[256,384]{0,1:T(8,128)S(1)}, f32[256,384]{0,1:T(8,128)}, u32[]{:S(2)}) copy-start(f32[256,384]{0,1:T(8,128)} %get-tuple-element.78) | copy-start | bytes 1179652
  388.4 26.5 %copy-start.14 = (f32[256,256]{1,0:T(8,128)}, f32[256,256]{1,0:T(8,128)S(1)}, u32[]{:S(2)}) copy-start(f32[256,256]{1,0:T(8,128)S(1)} %get-tuple-element.91) | copy-start | bytes 786436
  395.2 21.2 %copy-start.5 = (f32[256,256]{1,0:T(8,128)}, f32[256,256]{1,0:T(8,128)S(1)}, u32[]{:S(2)}) copy-start(f32[256,256]{1,0:T(8,128)S(1)} %get-tuple-element.210) | copy-start | bytes 786436
  395.2 21.2 %copy-start.23 = (s32[2,2]{1,0:T(2,128)}, s32[2,2]{1,0:T(2,128)S(1)}, u32[]{:S(2)}) copy-start(s32[2,2]{1,0:T(2,128)S(1)} %get-tuple-element.235) | copy-start | bytes 52
  414.9 1.5 copy-start.10
  414.9 2.2 copy-start.1
  416.4 0.7 copy-start.8
  429.5 4.3 copy-start.11
  429.5 4.3 copy-start.20
  429.5 25.7 %all-to-all-start.1 = ((f32[16,48,256]{2,1,0:T(8,128)}), f32[16,48,256]{2,1,0:T(8,128)S(1)}, u32[]{:S(2)}, u32[]{:S(2)}) async-start(f32[16,48,256]{2,1,0:T(8,128)} %reduce_sum.27), calls=%async_computation.1 | async-start | bytes 1572864 | tf_op jit(solution)/shard_map/all_to_all | solution.py:51
  434.2 26.6 %copy-start.6 = (f32[256,256]{1,0:T(8,128)S(1)}, f32[256,256]{1,0:T(8,128)}, u32[]{:S(2)}) copy-start(f32[256,256]{1,0:T(8,128)} %copy-done.5) | copy-start | bytes 786436
  456.3 25.9 %all-to-all-start.2 = ((f32[16,48,256]{2,1,0:T(8,128)}), f32[16,48,256]{2,1,0:T(8,128)}, u32[]{:S(2)}, u32[]{:S(2)}) async-start(f32[16,48,256]{2,1,0:T(8,128)} %broadcast_in_dim.49), calls=%async_computation.2 | async-start | bytes 1572864 | tf_op jit(solution)/shard_map/all_to_all | solution.py:56
  462.3 13.9 %copy-start.13 = (f32[256,128]{0,1:T(8,128)}, f32[256,128]{0,1:T(8,128)S(1)}, u32[]{:S(2)}) copy-start(f32[256,128]{0,1:T(8,128)S(1)} %fusion.42) | copy-start | bytes 393220
  462.9 0.7 copy-start.17
  476.2 0.9 copy-start.12
  493.1 79.9 %all-to-all-start.4 = ((f32[8,256,256]{2,1,0:T(8,128)}), f32[8,256,256]{2,1,0:T(8,128)}, u32[]{:S(2)}, u32[]{:S(2)}) async-start(f32[8,256,256]{2,1,0:T(8,128)} %broadcast_in_dim.51), calls=%async_computation.4 | async-start | bytes 4194304 | tf_op jit(solution)/shard_map/all_to_all | solution.py:56
  498.6 174.5 %all-gather.6.cloned.1.call-start = ((), (), s32[]{:S(2)}) async-start(), calls=%async_computation.7 | async-start | bytes 3538944 | tf_op jit(solution)/shard_map/all_gather | solution.py:87
  563.6 4.4 copy-start.18
  569.7 0.7 copy-start.7
  573.0 5.3 copy-start.4
  581.0 1.2 copy-start.2
  673.1 4.3 copy-start.3
  673.1 4.3 copy-start.9
  677.5 2.2 copy-start.16
  679.7 1.1 copy-start.15
  679.7 1.1 copy-start.22
Sparse Core Ops, SparseCore 0:
  13.1 146.5 reduce-scatter.3
  161.6 61.0 all-gather.3
  227.7 46.9 all-reduce.6
  277.3 75.1 all-reduce.8
  583.1 89.9 all-gather.5
